TPU v7x, 32 devices: a whole 2x2x4 slice. The times are simulated.
32 devices in a mesh: area: 8 (over z, y), tie: 4 (over x, core).
Axes of the slice: x: 2, y: 2, z: 4, core: 2. Of those that a mesh axis runs over, the one named last changes fastest.
Arguments:
- ginv: bfloat16 [128, 1024, 1024], P(('area', 'tie'))
- rhs: float32 [131072, 128], P(('area', 'tie')), may hold values from -6 to 6
- bnd_row: int32 [128, 128], P(('area', 'tie')), may hold values from -1 to 1023, as said below
- bnd_var: int32 [128, 128], P(('area', 'tie')), may hold values from -1 to 2047, as said below
Outputs:
- states: float32 [131072, 128], P(('area', 'tie'))
- consensus: float32 [2048, 128], P(('area', 'tie'))
- dual_value: float32 [16384, 128], P(('area', 'tie'))
Inputs may be any that keep to these rules, and one draw needn't show every extreme that they name: `bnd_row`: -1 marks an unused entry slot; the live rows of one area are distinct. `bnd_var`: -1 exactly where bnd_row is -1. Variable v is owned by the device holding rows v of the consensus output, block v // 64. The areas of one device hold at most 4 live entries owned by any one device; in every draw some owner holds exactly 4 from every device.
All inputs are finite; a program needn't handle non-finite values.
Results may differ from a plain program's by a relative error of at most 0.003.
Values sent between devices are 32-bit elements; how exact they have to be, the bound alone decides.
A program may use at most 64 MiB of HBM per device.

v0:
```python
import functools

import jax
import jax.numpy as jnp
from jax import lax
from jax.experimental import pallas as pl
from jax.experimental.pallas import tpu as pltpu
from jax.sharding import PartitionSpec as P

SLOT = 4
VAR_DEV = 64
ITERS = 4
PENALTY = 1.0

MESH = pl.DeviceIdType.MESH
F32 = jnp.float32
BF16 = jnp.bfloat16


def mm(a, b):
    return jnp.dot(a, b, preferred_element_type=F32)


def dot_dims(a, b, da, db):
    return lax.dot_general(a, b, (((da,), (db,)), ((), ())), preferred_element_type=F32)


def parts(x):
    high = x.astype(BF16)
    rest = x - high.astype(F32)
    mid = rest.astype(BF16)
    low = (rest - mid.astype(F32)).astype(BF16)
    return high, mid, low


def mm_parts(onehot, x):
    high, mid, low = parts(x)
    return mm(onehot, high) + (mm(onehot, mid) + mm(onehot, low))


def kernel(
    area_n,
    tie_n,
    srow_col,
    srow_lane,
    svar_col,
    g_hbm,
    rhs_hbm,
    states_ref,
    cons_ref,
    dual_ref,
    g_ref,
    rhs_ref,
    pick,
    out_buf,
    in_buf,
    rhs_b,
    y_base,
    g_bb,
    load_sem,
    send_sem,
    recv_sem,
):
    devices = area_n * tie_n
    area_dev, state_size, _ = g_ref.shape
    cap = devices * SLOT
    snap = dual_ref.shape[1]
    me_a, me_t = lax.axis_index("area"), lax.axis_index("tie")
    me = me_a * tie_n + me_t

    blocks = 4 if devices % 4 == 0 else 1
    block = devices // blocks
    me_block, me_in = me // block, lax.rem(me, block)
    upper = 2 * me_block >= blocks
    turned = jnp.where(upper, me_block, blocks - 1 - me_block)

    def peer_of(k):
        peer = lax.rem(me + k, devices)
        return peer, (peer // tie_n, lax.rem(peer, tie_n))

    barrier = pltpu.get_barrier_semaphore()

    @pl.loop(1, devices)
    def _(k):
        _, device = peer_of(k)
        pl.semaphore_signal(barrier, inc=1, device_id=device, device_id_type=MESH)

    def g_load(a):
        return pltpu.make_async_copy(g_hbm.at[a], g_ref.at[a], load_sem.at[0, a])

    def rhs_load(a):
        return pltpu.make_async_copy(rhs_hbm.at[a], rhs_ref.at[a], load_sem.at[1, a])

    for a in range(area_dev):
        g_load(a).start()
        rhs_load(a).start()

    def send(phase, value):
        out_buf[phase] = value.reshape(devices, SLOT, snap)
        in_buf[phase, me] = out_buf[phase, me]

        def post(peer):
            pltpu.make_async_remote_copy(
                src_ref=out_buf.at[phase, peer],
                dst_ref=in_buf.at[phase, me],
                send_sem=send_sem.at[phase],
                recv_sem=recv_sem.at[phase],
                device_id=(peer // tie_n, lax.rem(peer, tie_n)),
                device_id_type=MESH,
            ).start()

        @pl.loop(0, blocks - 1)
        def _(b):
            placed = b + jnp.where(b >= turned, 1, 0)
            base = jnp.where(upper, placed, blocks - 1 - placed) * block
            for i in range(block):
                post(base + lax.rem(me_in + i, block))

        for i in range(1, block):
            post(me_block * block + lax.rem(me_in + i, block))

    def receive(phase):
        span = in_buf.at[phase, pl.ds(0, devices - 1)]
        pltpu.make_async_copy(span, span, recv_sem.at[phase]).wait()
        return in_buf[phase].reshape(cap, snap)

    lane = lax.broadcasted_iota(jnp.int32, (cap, snap), 1)
    member_out = (svar_col[...] == lane).astype(F32)
    pl.semaphore_wait(barrier, devices - 1)
    send(0, member_out)

    rhs_b[...] = jnp.zeros_like(rhs_b)
    y_base[...] = jnp.zeros_like(y_base)
    g_bb[...] = jnp.zeros_like(g_bb)

    @pl.loop(0, area_dev)
    def _(a):
        column = lax.broadcasted_iota(jnp.int32, (cap, state_size), 1) + a * state_size
        chosen = (jnp.broadcast_to(srow_col[:, :1], (cap, state_size)) == column).astype(F32)
        chosen = chosen.astype(BF16)
        line = lax.broadcasted_iota(jnp.int32, (state_size, cap), 0) + a * state_size
        pick[a] = (
            (jnp.broadcast_to(srow_lane[:1, :], (state_size, cap)) == line)
            .astype(F32)
            .astype(BF16)
        )
        rhs_load(a).wait()
        high, mid, low = parts(rhs_ref[a])
        rhs_b[...] += mm(chosen, high) + (mm(chosen, mid) + mm(chosen, low))
        g_load(a).wait()
        rows = mm(chosen, g_ref[a]).astype(BF16)
        y_base[...] += mm(rows, high)
        g_bb[...] += mm(rows, pick[a])

    inner = g_bb[...].astype(BF16)
    own = rhs_b[...]
    first = y_base[...]
    steady = first - mm(inner, own.astype(BF16))

    member = receive(0).astype(BF16)
    same = dot_dims(member, member, 1, 1)
    share = 1.0 / jnp.maximum(jnp.sum(same, axis=1, keepdims=True), 1.0)
    same = same.astype(BF16)
    dual = jnp.zeros((cap, snap), F32)
    update = jnp.zeros((cap, snap), F32)
    for it in range(ITERS):
        if it == 0:
            local = first
        else:
            blended = (own + PENALTY * update).astype(BF16)
            local = steady + mm(inner, blended) + dual
        send(1 + 2 * it, local)
        if it == ITERS - 1:
            moved = parts(update)

            @pl.loop(0, area_dev)
            def _(a):
                scattered = mm(pick[a], moved[0]) + (mm(pick[a], moved[1]) + mm(pick[a], moved[2]))
                mixed = (rhs_ref[a] + PENALTY * scattered).astype(BF16)
                states_ref[a] = mm(g_ref[a], mixed)

        incoming = receive(1 + 2 * it)
        send(2 + 2 * it, mm_parts(same, incoming) * share)
        if it == ITERS - 1:
            high, mid, low = parts(incoming)
            totals = dot_dims(member, high, 0, 0) + (
                dot_dims(member, mid, 0, 0) + dot_dims(member, low, 0, 0)
            )
            counts = dot_dims(member, jnp.ones((cap, snap), BF16), 0, 0)
            consensus = totals * (1.0 / jnp.maximum(counts, 1.0))
            cons_ref[...] = consensus[: cons_ref.shape[0]]
        agreed = receive(2 + 2 * it)
        dual = local - agreed
        update = agreed - dual
    dual_ref[...] = dual

    for phase in range(1 + 2 * ITERS):
        span = out_buf.at[phase, pl.ds(0, devices - 1)]
        pltpu.make_async_copy(span, span, send_sem.at[phase]).wait()


def on_device(ginv, rhs, bnd_row, bnd_var):
    area_dev, state_size, _ = ginv.shape
    snap = rhs.shape[1]
    bound_size = bnd_row.shape[1]
    entries = area_dev * bound_size
    area_n = lax.axis_size("area")
    tie_n = lax.axis_size("tie")
    devices = area_n * tie_n
    cap = devices * SLOT
    row_flat = bnd_row.reshape(entries)
    var_flat = bnd_var.reshape(entries)
    active = row_flat >= 0
    order = jnp.arange(entries, dtype=jnp.int32)
    state_row = (order // bound_size) * state_size + row_flat
    owners = jnp.where(active, var_flat // VAR_DEV, devices)
    owned = owners[:, None] == jnp.arange(devices, dtype=jnp.int32)[None, :]
    earlier = (order[:, None] > order[None, :]).astype(BF16)
    before = mm(earlier, owned.astype(BF16))
    placed = jnp.sum(jnp.where(owned, before, 0.0), axis=1).astype(jnp.int32)
    slot = jnp.where(active, owners * SLOT + placed, -1)
    slots = jnp.arange(cap, dtype=jnp.int32)
    held = slots[:, None] == slot[None, :]
    srow = jnp.sum(jnp.where(held, (state_row + 1)[None, :], 0), axis=1) - 1
    svar = jnp.sum(jnp.where(held, (var_flat % VAR_DEV + 1)[None, :], 0), axis=1) - 1
    phases = 1 + 2 * ITERS
    vmem = pl.BlockSpec(memory_space=pltpu.VMEM)
    hbm = pl.BlockSpec(memory_space=pl.ANY)
    states, consensus, dual = pl.pallas_call(
        functools.partial(kernel, area_n, tie_n),
        out_shape=(
            jax.ShapeDtypeStruct((area_dev, state_size, snap), F32),
            jax.ShapeDtypeStruct((VAR_DEV, snap), F32),
            jax.ShapeDtypeStruct((cap, snap), F32),
        ),
        in_specs=[vmem, vmem, vmem, hbm, hbm],
        out_specs=(vmem, vmem, vmem),
        scratch_shapes=[
            pltpu.VMEM(ginv.shape, BF16),
            pltpu.VMEM((area_dev, state_size, snap), F32),
            pltpu.VMEM((area_dev, state_size, cap), BF16),
            pltpu.VMEM((phases, devices, SLOT, snap), F32),
            pltpu.VMEM((phases, devices, SLOT, snap), F32),
            pltpu.VMEM((cap, snap), F32),
            pltpu.VMEM((cap, snap), F32),
            pltpu.VMEM((cap, cap), F32),
            pltpu.SemaphoreType.DMA((2, area_dev)),
            pltpu.SemaphoreType.DMA((phases,)),
            pltpu.SemaphoreType.DMA((phases,)),
        ],
        compiler_params=pltpu.CompilerParams(
            collective_id=0, has_side_effects=True, vmem_limit_bytes=48 * 1024 * 1024
        ),
        name="admm",
    )(
        jnp.broadcast_to(srow[:, None], (cap, snap)),
        jnp.broadcast_to(srow[None, :], (8, cap)),
        jnp.broadcast_to(svar[:, None], (cap, snap)),
        ginv,
        rhs.reshape(area_dev, state_size, snap),
    )
    spread = (slot[:, None] == slots[None, :]).astype(F32)
    dual = jnp.dot(spread, dual, precision=lax.Precision.HIGHEST)
    return (states.reshape(area_dev * state_size, snap), consensus, dual)


def solution(mesh):
    both = ("area", "tie")
    in_specs = (P(both, None, None), P(both, None), P(both, None), P(both, None))
    out_specs = (P(both, None), P(both, None), P(both, None))
    return jax.shard_map(
        on_device, mesh=mesh, in_specs=in_specs, out_specs=out_specs, check_vma=False
    )
```

profile of v0, /device:TPU:0, one launch (start us, length us, event | category | flops | bytes accessed | tf_op | source)
XLA Modules:
  0.0 56.6 jit_solution(10666070196102772151)
XLA Ops:
  0.6 0.7 %fusion.4 = (s32[512]{0:T(512)S(1)}, pred[512]{0:T(512)(128)(4,1)S(1)}, s32[512]{0:T(512)S(1)}, s32[512]{0:T(512)S(1)}) fusion(s32[4,128]{1,0:T(4,128)} %param.7, s32[4,128]{1,0:T(4,128)} %param.6), kind=kLoop, calls=%fused_computation.20 | loop fusion | flops 16896 | bytes 10752 | tf_op jit(solution)/shard_map/jit(_where)/select_n | solution.py:216
  1.3 0.3 fusion
  1.6 0.1 select_reduce_fusion
  1.8 0.1 broadcast_in_dim.59.srow_col
  1.9 0.1 broadcast_in_dim.62.svar_col
  1.9 0.0 copy-start
  1.9 1.6 %copy-done = f32[4096,128]{1,0:T(8,128)S(1)} copy-done((f32[4096,128]{1,0:T(8,128)S(1)}, f32[4096,128]{1,0:T(8,128)}, u32[]{:S(2)}) %copy-start) | copy-done | bytes 2097176
  3.5 50.1 %admm.1 = (f32[4,1024,128]{2,1,0:T(8,128)S(1)}, f32[64,128]{1,0:T(8,128)S(1)}, f32[128,128]{1,0:T(8,128)S(1)}) custom-call(s32[128,128]{1,0:T(8,128)S(1)} %broadcast_in_dim.59.srow_col, s32[8,128]{1,0:T(8,128)S(1)} %broadcast_in_dim.60.srow_lane, s32[128,128]{1,0:T(8,128)S(1)} %broadcast_in_dim.62.svar_col, bf16[4,1024,1024]{2,1,0:T(8,128)(2,1)} %g_hbm.1, ...), custom_call_target="tpu_custom_call" | custom-call | tf_op jit(solution)/shard_map/admm/pallas_call | solution.py:229
  53.7 1.0 %fusion.1 = f32[512,128]{1,0:T(8,128)} fusion(f32[128,128]{1,0:T(8,128)S(1)} %get-tuple-element.8, s32[512]{0:T(512)S(1)} %add_select_fusion.3), kind=kOutput, calls=%fused_computation.7 | convolution fusion | flops 100728832 | bytes 329728 | tf_op jit(solution)/shard_map/dot_general | solution.py:263
  54.7 1.3 %copy.9 = f32[4096,128]{1,0:T(8,128)} copy(f32[4096,128]{1,0:T(8,128)S(1)} %bitcast.30) | data formatting | bytes 4194304
  56.0 0.6 %copy.10 = f32[64,128]{1,0:T(8,128)} copy(f32[64,128]{1,0:T(8,128)S(1)} %get-tuple-element.21) | data formatting | bytes 65536
  (3 shorter events, 0.0 us)
Async XLA Ops:
  1.9 1.6 %copy-start = (f32[4096,128]{1,0:T(8,128)S(1)}, f32[4096,128]{1,0:T(8,128)}, u32[]{:S(2)}) copy-start(f32[4096,128]{1,0:T(8,128)} %param.5) | copy-start | bytes 6291460
where the time goes:
time: 56.8 us; the launch traced here: 56.6 us
  Pallas kernels  50.1 us (88%)
  local copies, waits for them, and re-layouts  3.69 us (6%)
  matrix products  1.3 us (2%)
  other arithmetic  0.85 us (1%)
  between operations  0.67 us (1%)
    pallas_call x1, Pallas kernels, on_device(): pl.pallas_call(functools.partial(kernel, area_n, tie_n), out_shape=(jax.S...  50.1 us
    unnamed x4, local copies, waits for them, and re-layouts  3.53 us

commit v1 on v0

--- a/solution.py
+++ b/solution.py
@@ -264,10 +264,457 @@
     return (states.reshape(area_dev * state_size, snap), consensus, dual)
 
 
+def split(x):
+    high = x.astype(BF16)
+    return high, (x - high.astype(F32)).astype(BF16)
+
+
+def column_kernel(
+    ny,
+    area_n,
+    tie_n,
+    row_hbm,
+    var_hbm,
+    g_hbm,
+    rhs_hbm,
+    states_ref,
+    cons_ref,
+    dual_ref,
+    row_ref,
+    var_ref,
+    g_ref,
+    rhs_ref,
+    srow_col,
+    srow_lane,
+    hold_t,
+    weights,
+    g_cols,
+    own_ref,
+    first_ref,
+    k_ref,
+    sv_out,
+    sv_in,
+    x_out,
+    x_in,
+    u_out,
+    u_in,
+    f_out,
+    f_in,
+    k_buf,
+    k16,
+    same16,
+    var16,
+    share_ref,
+    count_ref,
+    lhs_ref,
+    res_ref,
+    load_sem,
+    index_sem,
+    barrier_done,
+    send_sem,
+    recv_sem,
+    k_send,
+    k_recv,
+    k_pair,
+):
+    del barrier_done
+    D = area_n * tie_n
+    area_dev, state_size, _ = g_ref.shape
+    bound = row_ref.shape[1]
+    cap = D * SLOT
+    snap = rhs_ref.shape[2]
+    cols = snap // D
+    nz = area_n // ny
+    var_dev = cons_ref.shape[0]
+    me_a, me_t = lax.axis_index("area"), lax.axis_index("tie")
+    me = me_a * tie_n + me_t
+    z, y, x, c = me_a // ny, lax.rem(me_a, ny), me_t // 2, lax.rem(me_t, 2)
+
+    def place(px, py, pz, pc):
+        return pz * ny + py, px * 2 + pc
+
+    def flat(px, py, pz, pc):
+        return (pz * ny + py) * tie_n + px * 2 + pc
+
+    barrier = pltpu.get_barrier_semaphore()
+
+    @pl.loop(1, D)
+    def _(k):
+        peer = lax.rem(me + k, D)
+        pl.semaphore_signal(
+            barrier, inc=1, device_id=(peer // tie_n, lax.rem(peer, tie_n)), device_id_type=MESH
+        )
+
+    def g_load(a):
+        return pltpu.make_async_copy(g_hbm.at[a], g_ref.at[a], load_sem.at[0, a])
+
+    def rhs_load(a):
+        return pltpu.make_async_copy(rhs_hbm.at[a], rhs_ref.at[a], load_sem.at[1, a])
+
+    row_load = pltpu.make_async_copy(row_hbm, row_ref, index_sem.at[0])
+    var_load = pltpu.make_async_copy(var_hbm, var_ref, index_sem.at[1])
+    row_load.start()
+    var_load.start()
+    for a in range(area_dev):
+        rhs_load(a).start()
+        g_load(a).start()
+
+    def exchange(out_buf, in_buf, phase):
+        in_buf[me] = out_buf[me]
+
+        @pl.loop(1, D)
+        def _(k):
+            peer = lax.rem(me + k, D)
+            pltpu.make_async_remote_copy(
+                src_ref=out_buf.at[peer],
+                dst_ref=in_buf.at[me],
+                send_sem=send_sem.at[phase],
+                recv_sem=recv_sem.at[phase],
+                device_id=(peer // tie_n, lax.rem(peer, tie_n)),
+                device_id_type=MESH,
+            ).start()
+
+    def arrived(in_buf, phase):
+        span = in_buf.at[pl.ds(0, D - 1)]
+        pltpu.make_async_copy(span, span, recv_sem.at[phase]).wait()
+
+    def sent(out_buf, phase):
+        span = out_buf.at[pl.ds(0, D - 1)]
+        pltpu.make_async_copy(span, span, send_sem.at[phase]).wait()
+
+    row_load.wait()
+    var_load.wait()
+    rows = row_ref[...]
+    variables = var_ref[...]
+    owner_line = lax.broadcasted_iota(jnp.int32, (D, bound), 0)
+    earlier = (
+        lax.broadcasted_iota(jnp.int32, (bound, bound), 0)
+        < lax.broadcasted_iota(jnp.int32, (bound, bound), 1)
+    )
+    earlier = earlier.astype(F32).astype(BF16)
+    slot_line = lax.broadcasted_iota(jnp.int32, (cap, bound), 0)
+    slot_lane = lax.broadcasted_iota(jnp.int32, (bound, cap), 1)
+    carry = jnp.zeros((D, 1), F32)
+    sv_col = jnp.zeros((cap, bound), F32)
+    slot_rows = []
+    for a in range(area_dev):
+        row, var = rows[a : a + 1], variables[a : a + 1]
+        live = row >= 0
+        owner = jnp.where(live, var // var_dev, D)
+        owned = (jnp.broadcast_to(owner, (D, bound)) == owner_line).astype(F32)
+        before = mm(owned.astype(BF16), earlier) + carry
+        carry = carry + jnp.sum(owned, axis=1, keepdims=True)
+        rank = jnp.sum(owned * before, axis=0, keepdims=True)
+        slot = jnp.where(live, rank.astype(jnp.int32) * D + owner, -1)
+        slot_rows.append(slot)
+        held = jnp.broadcast_to(slot, (cap, bound)) == slot_line
+        srow = jnp.sum(
+            jnp.where(held, jnp.broadcast_to(row + 1, (cap, bound)), 0).astype(F32),
+            axis=1,
+            keepdims=True,
+        )
+        srow_col[a] = jnp.broadcast_to(srow, (cap, bound)) - 1.0
+        sv_col = sv_col + jnp.where(
+            held, jnp.broadcast_to(lax.rem(var, var_dev) + 1, (cap, bound)), 0
+        ).astype(F32)
+    sv_wide = jnp.broadcast_to(jnp.sum(sv_col, axis=1, keepdims=True), (cap, bound)) - 1.0
+    sv_row = sv_wide.T[:1]
+    for a in range(area_dev):
+        srow_lane[a] = srow_col[a].T[:8]
+    slot_all = jnp.concatenate(slot_rows + [slot_rows[0]] * (8 - area_dev), axis=0).astype(F32)
+    slot_cols = jnp.concatenate([slot_all] * (bound // 8), axis=0).T
+    for a in range(area_dev):
+        column = jnp.broadcast_to(slot_cols[:, a : a + 1], (bound, cap))
+        hold_t[a] = (column == slot_lane.astype(F32)).astype(F32).astype(BF16)
+    sv_out[...] = jnp.broadcast_to(sv_row.reshape(1, 1, cap), (D, 1, cap))
+
+    pl.semaphore_wait(barrier, D - 1)
+    exchange(sv_out, sv_in, 0)
+
+    own_ref[...] = jnp.zeros_like(own_ref)
+    first_ref[...] = jnp.zeros_like(first_ref)
+    k_ref[...] = jnp.zeros_like(k_ref)
+
+    @pl.loop(0, area_dev)
+    def _(a):
+        column = lax.broadcasted_iota(jnp.int32, (cap, state_size), 1).astype(F32)
+        chosen = jnp.broadcast_to(srow_col[a][:, :1], (cap, state_size)) == column
+        chosen = chosen.astype(F32).astype(BF16)
+        line = lax.broadcasted_iota(jnp.int32, (state_size, cap), 0).astype(F32)
+        pick = jnp.broadcast_to(srow_lane[a][:1], (state_size, cap)) == line
+        weights[:, snap:] = pick.astype(F32).astype(BF16)
+        rhs_load(a).wait()
+        high, mid = split(rhs_ref[a])
+        weights[:, :snap] = high
+        own_ref[...] += mm(chosen, high) + mm(chosen, mid)
+        g_load(a).wait()
+        both = mm(g_ref[a], weights[...])
+        base = both[:, :snap]
+        columns = both[:, snap:].astype(BF16)
+        states_ref[a] = base
+        g_cols[a] = columns
+        high, mid = split(base)
+        first_ref[...] += mm(chosen, high) + mm(chosen, mid)
+        k_ref[...] += mm(chosen, columns)
+
+    own = own_ref[...]
+    k_buf[me] = k_ref[...].T
+
+    total = [0, 0]
+
+    def block(b, part):
+        half = cap // 2
+        return k_buf.at[b] if part is None else k_buf.at[b, pl.ds(part * half, half)]
+
+    def forward(b, part, device, sem):
+        ref = block(b, part)
+        total[0] += 2 if part is None else 1
+        pltpu.make_async_remote_copy(
+            src_ref=ref,
+            dst_ref=ref,
+            send_sem=k_send,
+            recv_sem=sem,
+            device_id=device,
+            device_id_type=MESH,
+        ).start()
+
+    def landed(b, part, sem):
+        ref = block(b, part)
+        pltpu.make_async_copy(ref, ref, sem).wait()
+
+    x_next, y_next, pair = place(1 - x, y, z, c), place(x, 1 - y, z, c), place(x, y, z, 1 - c)
+    heights = [lax.rem(z + k, nz) for k in range(nz)]
+
+    x_out[:, pl.ds(0, cols), :] = first_ref[...].T.reshape(D, cols, cap)
+    x_out[:, pl.ds(cols, cols), :] = own.T.reshape(D, cols, cap)
+    forward(me, None, x_next, k_recv.at[me, 0])
+    forward(me, None, y_next, k_recv.at[me, 0])
+    for k in range(1, nz):
+        forward(me, None, place(x, y, heights[k], c), k_recv.at[me, 0])
+    exchange(x_out, x_in, 1)
+    forward(me, None, pair, k_pair.at[me])
+
+    lane_block = lax.broadcasted_iota(jnp.int32, (D, cap), 1) // D
+
+    def shuffle(p):
+        turned = p.T
+        rolled = [turned] + [pltpu.roll(turned, k * D, 1) for k in range(1, SLOT)]
+        parts_out = []
+        for i in range(cols):
+            piece = rolled[(0 - i) % SLOT][:D]
+            for s in range(1, SLOT):
+                piece = jnp.where(
+                    lane_block == s, rolled[(s - i) % SLOT][s * D : (s + 1) * D], piece
+                )
+            parts_out.append(piece)
+        return jnp.concatenate(parts_out, axis=0)
+
+    arrived(sv_in, 0)
+    sv = sv_in[...].reshape(D, cap)
+    sv_q = shuffle(jnp.concatenate([sv] * cols, axis=0))
+    sv_t = sv_q.T
+    var_lane = lax.broadcasted_iota(jnp.int32, (cap, cap), 1).astype(F32)
+    for o in range(D):
+        column = jnp.broadcast_to(sv_t[:, o : o + 1], (cap, cap))
+        line = jnp.broadcast_to(sv_q[o : o + 1], (cap, cap))
+        equal = ((column == line) & (line >= 0.0)).astype(F32)
+        hit = (column == var_lane).astype(F32)
+        same16[o] = equal.astype(BF16)
+        var16[o] = hit.astype(BF16)
+        share_ref[pl.ds(o, 1)] = 1.0 / jnp.maximum(jnp.sum(equal, axis=0, keepdims=True), 1.0)
+        count_ref[pl.ds(o, 1)] = 1.0 / jnp.maximum(jnp.sum(hit, axis=0, keepdims=True), 1.0)
+
+    for k in range(1, nz):
+        b = flat(x, y, heights[k], c)
+        landed(b, None, k_recv.at[b, 0])
+        forward(b, None, x_next, k_recv.at[b, 0])
+        forward(b, None, y_next, k_recv.at[b, 0])
+        forward(b, None, pair, k_pair.at[b])
+
+    def put(ref, base, value):
+        for i in range(cols):
+            ref[:, base + i, :] = value[i * D : (i + 1) * D]
+
+    def get(ref, base):
+        return jnp.concatenate([ref[:, base + i, :] for i in range(cols)], axis=0)
+
+    share = jnp.concatenate([share_ref[...]] * cols, axis=0)
+
+    def average(local, last):
+        q = shuffle(local)
+        high = q.astype(BF16).astype(F32)
+        put(lhs_ref, 0, high)
+        put(lhs_ref, cols, q - high)
+        for o in range(D):
+            left = lhs_ref[o].astype(BF16)
+            res_ref[o] = mm(left, same16[o])
+            if last:
+                both = mm(left, var16[o])
+                f_out[o, pl.ds(cols, cols)] = (both[:cols] + both[cols:]) * count_ref[pl.ds(o, 1)]
+        return shuffle((get(res_ref, 0) + get(res_ref, cols)) * share)
+
+    arrived(x_in, 1)
+    first = get(x_in, 0)
+    own_p = get(x_in, cols)
+    local = first
+    agreed = average(local, False)
+    dual = local - agreed
+    update = agreed - dual
+
+    for k in range(nz):
+        bx, by = flat(1 - x, y, heights[k], c), flat(x, 1 - y, heights[k], c)
+        landed(bx, None, k_recv.at[bx, 0])
+        forward(bx, 0, y_next, k_recv.at[bx, 0])
+        forward(bx, None, pair, k_pair.at[bx])
+        landed(by, None, k_recv.at[by, 0])
+        forward(by, 1, x_next, k_recv.at[by, 1])
+        forward(by, None, pair, k_pair.at[by])
+    for k in range(nz):
+        b = flat(1 - x, 1 - y, heights[k], c)
+        landed(b, 0, k_recv.at[b, 0])
+        landed(b, 1, k_recv.at[b, 1])
+        forward(b, None, pair, k_pair.at[b])
+    for px in range(2):
+        for py in range(ny):
+            for pz in range(nz):
+                b = flat(px, py, pz, 1 - c)
+                landed(b, None, k_pair.at[b])
+
+    put(lhs_ref, 0, own_p)
+    put(lhs_ref, cols, own_p + PENALTY * update)
+    for d in range(D):
+        k16[d] = k_buf[d].astype(BF16)
+        res_ref[d] = mm(lhs_ref[d].astype(BF16), k16[d])
+    steady = first - get(res_ref, 0)
+    local = steady + get(res_ref, cols) + dual
+
+    for it in range(1, ITERS):
+        agreed = average(local, it == ITERS - 1)
+        dual = local - agreed
+        update = agreed - dual
+        if it == ITERS - 1:
+            put(f_out, 0, dual)
+            exchange(f_out, f_in, 3)
+            break
+        if it == ITERS - 2:
+            put(u_out, 0, update)
+            exchange(u_out, u_in, 2)
+        put(lhs_ref, 0, own_p + PENALTY * update)
+        for d in range(D):
+            res_ref[d] = mm(lhs_ref[d].astype(BF16), k16[d])
+        local = steady + get(res_ref, 0) + dual
+
+    arrived(u_in, 2)
+    final = u_in[...].reshape(snap, cap).T
+    moved = (own + PENALTY * final).astype(BF16).astype(F32) - own.astype(BF16).astype(F32)
+    high, mid = split(moved)
+
+    @pl.loop(0, area_dev)
+    def _(a):
+        states_ref[a] += mm(g_cols[a], high) + mm(g_cols[a], mid)
+
+    arrived(f_in, 3)
+    dual = f_in[:, pl.ds(0, cols), :].reshape(snap, cap).T
+    high, mid = split(dual)
+    for a in range(area_dev):
+        dual_ref[pl.ds(a * bound, bound)] = mm(hold_t[a], high) + mm(hold_t[a], mid)
+    consensus = f_in[:, pl.ds(cols, cols), :].reshape(snap, cap).T
+    cons_ref[...] = consensus[:var_dev]
+
+    sent(sv_out, 0)
+    sent(x_out, 1)
+    sent(u_out, 2)
+    sent(f_out, 3)
+    whole = k_buf.at[0]
+    for _ in range(total[0] // 2):
+        pltpu.make_async_copy(whole, whole, k_send).wait()
+    if total[0] % 2:
+        landed(0, 0, k_send)
+
+
+def on_device_columns(ginv, rhs, bnd_row, bnd_var):
+    area_dev, state_size, _ = ginv.shape
+    snap = rhs.shape[1]
+    bound = bnd_row.shape[1]
+    area_n = lax.axis_size("area")
+    tie_n = lax.axis_size("tie")
+    D = area_n * tie_n
+    cap = D * SLOT
+    cols = snap // D
+    ny = tie_n // 2
+    vmem = pl.BlockSpec(memory_space=pltpu.VMEM)
+    hbm = pl.BlockSpec(memory_space=pltpu.HBM)
+    V = pltpu.VMEM
+    states, consensus, dual = pl.pallas_call(
+        functools.partial(column_kernel, ny, area_n, tie_n),
+        out_shape=(
+            jax.ShapeDtypeStruct((area_dev, state_size, snap), F32),
+            jax.ShapeDtypeStruct((VAR_DEV, snap), F32),
+            jax.ShapeDtypeStruct((area_dev * bound, snap), F32),
+        ),
+        in_specs=[hbm] * 4,
+        out_specs=(vmem, vmem, vmem),
+        scratch_shapes=[
+            V((area_dev, bound), jnp.int32),
+            V((area_dev, bound), jnp.int32),
+            V(ginv.shape, BF16),
+            V((area_dev, state_size, snap), F32),
+            V((area_dev, cap, bound), F32),
+            V((area_dev, 8, cap), F32),
+            V((area_dev, bound, cap), BF16),
+            V((state_size, snap + cap), BF16),
+            V((area_dev, state_size, cap), BF16),
+            V((cap, snap), F32),
+            V((cap, snap), F32),
+            V((cap, cap), F32),
+            V((D, 1, cap), F32),
+            V((D, 1, cap), F32),
+            V((D, 2 * cols, cap), F32),
+            V((D, 2 * cols, cap), F32),
+            V((D, cols, cap), F32),
+            V((D, cols, cap), F32),
+            V((D, 2 * cols, cap), F32),
+            V((D, 2 * cols, cap), F32),
+            V((D, cap, cap), F32),
+            V((D, cap, cap), BF16),
+            V((D, cap, cap), BF16),
+            V((D, cap, cap), BF16),
+            V((D, cap), F32),
+            V((D, cap), F32),
+            V((D, 2 * cols, cap), F32),
+            V((D, 2 * cols, cap), F32),
+            pltpu.SemaphoreType.DMA((2, area_dev)),
+            pltpu.SemaphoreType.DMA((2,)),
+            pltpu.SemaphoreType.DMA,
+            pltpu.SemaphoreType.DMA((4,)),
+            pltpu.SemaphoreType.DMA((4,)),
+            pltpu.SemaphoreType.DMA,
+            pltpu.SemaphoreType.DMA((D, 2)),
+            pltpu.SemaphoreType.DMA((D,)),
+        ],
+        compiler_params=pltpu.CompilerParams(
+            collective_id=0, has_side_effects=True, vmem_limit_bytes=56 * 1024 * 1024
+        ),
+        name="admm_columns",
+    )(bnd_row, bnd_var, ginv, rhs.reshape(area_dev, state_size, snap))
+    return (states.reshape(area_dev * state_size, snap), consensus, dual)
+
+
+def columns_fit(mesh, snap):
+    area_n, tie_n = mesh.shape["area"], mesh.shape["tie"]
+    cap = area_n * tie_n * SLOT
+    return tie_n == 4 and area_n % 2 == 0 and snap == cap == 128
+
+
+def on_any_device(mesh, ginv, rhs, bnd_row, bnd_var):
+    step = on_device_columns if columns_fit(mesh, rhs.shape[1]) else on_device
+    return step(ginv, rhs, bnd_row, bnd_var)
+
+
 def solution(mesh):
     both = ("area", "tie")
     in_specs = (P(both, None, None), P(both, None), P(both, None), P(both, None))
     out_specs = (P(both, None), P(both, None), P(both, None))
     return jax.shard_map(
-        on_device, mesh=mesh, in_specs=in_specs, out_specs=out_specs, check_vma=False
+        functools.partial(on_any_device, mesh), mesh=mesh, in_specs=in_specs, out_specs=out_specs, check_vma=False
     )

time: 56.8 us -> 50.9 us (0.90)
  Pallas kernels: 50.1 us -> 45.7 us
  matrix products: 1.3 us -> 0 us
  other arithmetic: 0.85 us -> 0 us
  local copies, waits for them, and re-layouts: 3.69 us -> 4.41 us
    pallas_call x1, Pallas kernels: 50.1 us -> 45.7 us  [on_device_columns(): pl.pallas_call(functools.partial(column_kernel, ny, area_n, tie_n), out_s...]
    dot_general x2 -> x0, matrix products: 1.3 us -> none  [the longest x1 1.03 us: on_device(): dual = jnp.dot(spread, dual, precision=lax.Precision.HIGHEST)]
    unnamed x4 -> x7, local copies, waits for them, and re-layouts: 3.53 us -> 4.41 us
    select_n x2 -> x0, other arithmetic: 0.72 us -> none  [the longest x1 0.71 us: on_device(): owners = jnp.where(active, var_flat // VAR_DEV, devices)]
where the time goes in v1:
time: 50.9 us; the launch traced here: 50.8 us
  Pallas kernels  45.7 us (90%)
  local copies, waits for them, and re-layouts  4.41 us (9%)
  between operations  0.66 us (1%)
    pallas_call x1, Pallas kernels, on_device_columns(): pl.pallas_call(functools.partial(column_kernel, ny, area_n, tie_n), out_s...  45.7 us
    unnamed x7, local copies, waits for them, and re-layouts  4.41 us

profile of v1, /device:TPU:0, one launch (start us, length us, event | category | flops | bytes accessed | tf_op | source)
XLA Modules:
  0.0 50.8 jit_solution(13818223009443258186)
XLA Ops:
  0.6 45.7 %admm_columns.1 = (f32[4,1024,128]{2,1,0:T(8,128)}, f32[64,128]{1,0:T(8,128)}, f32[512,128]{1,0:T(8,128)}) custom-call(s32[4,128]{1,0:T(4,128)} %row_hbm.1, s32[4,128]{1,0:T(4,128)} %var_hbm.1, bf16[4,1024,1024]{2,1,0:T(8,128)(2,1)} %g_hbm.1, f32[4,1024,128]{2,1,0:T(8,128)} %bitcast.2), custom_call_target="tpu_custom_call" | custom-call | tf_op jit(solution)/shard_map/admm_columns/pallas_call | solution.py:648
  46.3 0.0 copy-start.1
  46.4 0.0 copy-start
  46.4 3.1 %copy.10 = f32[4096,128]{1,0:T(8,128)} copy(f32[4096,128]{1,0:T(8,128)} %bitcast.3) | data formatting | bytes 4194304
  49.5 0.0 copy-done.1
  49.5 0.6 %copy.11 = f32[64,128]{1,0:T(8,128)} copy(f32[64,128]{1,0:T(8,128)S(1)} %copy-done.1) | data formatting | bytes 65536
  50.1 0.0 copy-done
  50.1 0.7 %copy.12 = f32[512,128]{1,0:T(8,128)} copy(f32[512,128]{1,0:T(8,128)S(1)} %copy-done) | data formatting | bytes 524288
Async XLA Ops:
  46.3 3.1 %copy-start.1 = (f32[64,128]{1,0:T(8,128)S(1)}, f32[64,128]{1,0:T(8,128)}, u32[]{:S(2)}) copy-start(f32[64,128]{1,0:T(8,128)} %get-tuple-element.13) | copy-start | bytes 98308
  46.4 3.7 %copy-start = (f32[512,128]{1,0:T(8,128)S(1)}, f32[512,128]{1,0:T(8,128)}, u32[]{:S(2)}) copy-start(f32[512,128]{1,0:T(8,128)} %get-tuple-element.14) | copy-start | bytes 786436
